TPU v7x, 32 devices: a whole 2x2x4 slice. The times are simulated.
32 devices in a mesh: row: 4 (over z), col: 4 (over y, x), layer: 2 (over core).
Axes of the slice: x: 2, y: 2, z: 4, core: 2. Of those that a mesh axis runs over, the one named last changes fastest.
Arguments:
- basis: float32 [4096, 4096], P('row', 'col'), may hold values from -1 to 1, as said below
- basis_grad: float32 [4096, 4096], P('row', 'col'), may hold values from -768 to 768
- value_grad: float32 [4096], replicated, may hold values from -384 to 384
- ranks: int32 [4096], replicated, may hold values from 0 to 4095, each once
- offsets: int32 [4096], replicated, may hold values from 0 to 3
Outputs:
- grad_matrix: float32 [4096, 4096], P(('row', 'layer'), 'col')
Inputs may be any that keep to these rules, and one draw needn't show every extreme that they name: The columns of basis are orthonormal. ranks holds every number of 0 to 4095 once, so eigenvalues of different indices differ by 1 or more.
All inputs are finite; a program needn't handle non-finite values.
Results may differ from a plain program's by a relative error of at most 0.000098.
Values sent between devices are 32-bit elements; how exact they have to be, the bound alone decides.
A program may use at most 128 MiB of HBM per device.

v0:
```python
import jax
import jax.numpy as jnp
from jax import lax
from jax.sharding import PartitionSpec as P


def on_device(basis, basis_grad, value_grad, ranks, offsets):
    highest = lax.Precision.HIGHEST
    rows_blk, cols_blk = basis.shape
    layers = lax.axis_size("layer")
    row_id = lax.axis_index("row")
    col_id = lax.axis_index("col")
    layer_id = lax.axis_index("layer")
    half_rows = rows_blk // layers
    half_cols = cols_blk // layers
    u_top = lax.dynamic_slice_in_dim(basis, layer_id * half_rows, half_rows, 0)
    du_top = lax.dynamic_slice_in_dim(basis_grad, layer_id * half_rows, half_rows, 0)
    row_strip = lax.all_gather(u_top, "col", axis=1, tiled=True)
    mirrored = lax.all_to_all(row_strip, "row", split_axis=1, concat_axis=0, tiled=True)
    section = mirrored
    inner = lax.dot_general(
        section,
        lax.all_gather(du_top, "row", axis=0, tiled=True),
        (((0,), (0,)), ((), ())),
        precision=highest,
        preferred_element_type=jnp.float32,
    )
    inner_whole = lax.psum(inner, "layer")
    inner_half = lax.dynamic_slice_in_dim(inner_whole, layer_id * half_rows, half_rows, 0)
    eigen = 4.0 * ranks.astype(jnp.float32) + offsets.astype(jnp.float32)
    row_begin = row_id * rows_blk + layer_id * half_rows
    col_begin = col_id * cols_blk
    row_index = row_begin + jnp.arange(half_rows, dtype=jnp.int32)
    col_index = col_begin + jnp.arange(cols_blk, dtype=jnp.int32)
    eigen_rows = lax.dynamic_slice_in_dim(eigen, row_begin, half_rows, 0)
    eigen_cols = lax.dynamic_slice_in_dim(eigen, col_begin, cols_blk, 0)
    grad_cols = lax.dynamic_slice_in_dim(value_grad, col_begin, cols_blk, 0)
    on_diagonal = row_index[:, None] == col_index[None, :]
    spacing = eigen_cols[None, :] - eigen_rows[:, None]
    scaled = jnp.where(
        on_diagonal,
        grad_cols[None, :],
        inner_half / jnp.where(on_diagonal, jnp.float32(1.0), spacing),
    )
    u_right = lax.dynamic_slice_in_dim(basis, layer_id * half_cols, half_cols, 1)
    u_strip = lax.all_gather(u_right, "col", axis=1, tiled=True)
    section = u_strip
    left_prod = jnp.dot(
        section,
        lax.all_gather(scaled, "row", axis=0, tiled=True),
        precision=highest,
        preferred_element_type=jnp.float32,
    )
    left_whole = lax.psum(left_prod, "layer")
    left_half = lax.dynamic_slice_in_dim(left_whole, layer_id * half_cols, half_cols, 1)
    column_slab = lax.all_gather(u_right, "row", axis=0, tiled=True)
    far_rows = lax.all_to_all(column_slab, "col", split_axis=0, concat_axis=1, tiled=True)
    section = far_rows
    product = lax.dot_general(
        lax.all_gather(left_half, "col", axis=1, tiled=True),
        section,
        (((1,), (1,)), ((), ())),
        precision=highest,
        preferred_element_type=jnp.float32,
    )
    product_whole = lax.psum(product, "layer")
    return lax.dynamic_slice_in_dim(product_whole, layer_id * half_rows, half_rows, 0)


def solution(mesh):
    placed = (P("row", "col"), P("row", "col"), P(), P(), P())
    return jax.shard_map(
        on_device, mesh=mesh, in_specs=placed, out_specs=P(("row", "layer"), "col"), check_vma=False
    )
```

profile of v0, /device:TPU:0, one launch (start us, length us, event | category | flops | bytes accessed | tf_op | source)
XLA Modules:
  0.0 1150.9 jit_solution(15944361618842330479)
XLA Ops:
  7.4 1.7 constant_dynamic-slice_fusion.3
  9.1 1.8 copy.9
  10.9 90.4 %all-gather.9.cloned.1.call-done = f32[512,4096]{0,1:T(8,128)} async-done(((f32[512,1024]{0,1:T(8,128)}), f32[512,4096]{0,1:T(8,128)}) %all-gather.9.cloned.1.call-update) | async-done | bytes 8388624 | tf_op jit(solution)/shard_map/all_gather | solution.py:18
  101.3 5.7 all-to-all-start
  107.1 3.2 constant_dynamic-slice_fusion.2
  110.3 314.7 %all-to-all-done = f32[512,4,1024]{0,2,1:T(8,128)} async-done(((f32[512,4,1024]{0,2,1:T(8,128)}), f32[512,4,1024]{0,2,1:T(8,128)}, u32[]{:S(2)}, u32[]{:S(2)}) %all-to-all-start) | async-done | bytes 8388640 | tf_op jit(solution)/shard_map/all_to_all | solution.py:19
  425.0 8.8 copy.7
  433.8 31.6 %fusion.1 = f32[1024,1024]{1,0:T(8,128)} fusion(f32[2048,1024]{1,0:T(8,128)} %bitcast.15, f32[2048,1024]{1,0:T(8,128)} %all-gather.11.cloned.1.call-done), kind=kOutput, calls=%fused_computation.11 | convolution fusion | flops 25769803776 | bytes 20971520 | tf_op jit(solution)/shard_map/dot_general | solution.py:21
  465.5 3.1 constant_dynamic-slice_fusion.4
  468.8 0.7 dynamic_slice.28
  469.5 22.3 %all-reduce.4.cloned.1.call-done = f32[1024,1024]{1,0:T(8,128)} async-done(((f32[1024,1024]{1,0:T(8,128)}), f32[1024,1024]{1,0:T(8,128)}) %all-reduce.4.cloned.1.call-update) | async-done | bytes 4194320 | tf_op jit(solution)/shard_map/psum | solution.py:28
  491.8 3.4 compare_select_fusion
  495.5 86.9 %all-gather.7.cloned.1.call-done = f32[1024,2048]{1,0:T(8,128)} async-done(((f32[1024,512]{1,0:T(8,128)}), f32[1024,2048]{1,0:T(8,128)}) %all-gather.7.cloned.1.call-update) | async-done | bytes 8388624 | tf_op jit(solution)/shard_map/all_gather | solution.py:46
  582.4 151.1 %all-gather.13.cloned.1.call-done = f32[2048,1024]{1,0:T(8,128)} async-done(((f32[512,1024]{1,0:T(8,128)}), f32[2048,1024]{1,0:T(8,128)}) %all-gather.13.cloned.1.call-update) | async-done | bytes 8388624 | tf_op jit(solution)/shard_map/all_gather | solution.py:50
  733.4 31.8 %fusion.2 = f32[1024,1024]{1,0:T(8,128)} fusion(f32[1024,2048]{1,0:T(8,128)} %all-gather.7.cloned.1.call-done, f32[2048,1024]{1,0:T(8,128)} %all-gather.13.cloned.1.call-done), kind=kOutput, calls=%fused_computation.12 | convolution fusion | flops 25769803776 | bytes 20971520 | tf_op jit(solution)/shard_map/dot_general | solution.py:48
  765.4 0.5 all-gather.17.cloned.1.call-update
  765.9 25.8 %all-reduce.6.cloned.1.call-done = f32[1024,1024]{1,0:T(8,128)} async-done(((f32[1024,1024]{1,0:T(8,128)}), f32[1024,1024]{1,0:T(8,128)}) %all-reduce.6.cloned.1.call-update) | async-done | bytes 4194320 | tf_op jit(solution)/shard_map/psum | solution.py:54
  791.7 3.2 constant_dynamic-slice_fusion.1
  795.0 120.1 %all-gather.17.cloned.1.call-done = f32[4096,512]{1,0:T(8,128)} async-done(((f32[1024,512]{1,0:T(8,128)}), f32[4096,512]{1,0:T(8,128)}) %all-gather.17.cloned.1.call-update) | async-done | bytes 8388624 | tf_op jit(solution)/shard_map/all_gather | solution.py:56
  915.1 158.6 %all_to_all.38 = f32[4,1024,512]{2,1,0:T(8,128)} all-to-all(f32[4,1024,512]{2,1,0:T(8,128)} %bitcast.13), channel_id=1, replica_groups=mesh['row'=4,'col'=4,'layer'=2] {'col'}, dimensions={0} | all-to-all | bytes 16777216 | tf_op jit(solution)/shard_map/all_to_all | solution.py:57
  1073.7 8.7 copy.8
  1082.8 31.8 %fusion.3 = f32[1024,1024]{1,0:T(8,128)} fusion(f32[1024,2048]{1,0:T(8,128)} %all-gather.15.cloned.1.call-done, f32[1024,2048]{0,1:T(8,128)} %bitcast.16), kind=kOutput, calls=%fused_computation.13 | convolution fusion | flops 25769803776 | bytes 20971520 | tf_op jit(solution)/shard_map/dot_general | solution.py:59
  1114.6 25.5 %all-reduce.8.cloned.1.call-done = f32[1024,1024]{1,0:T(8,128)} async-done(((f32[1024,1024]{1,0:T(8,128)}), f32[1024,1024]{1,0:T(8,128)}) %all-reduce.8.cloned.1.call-update) | async-done | bytes 4194320 | tf_op jit(solution)/shard_map/psum | solution.py:66
  1140.1 3.2 constant_dynamic-slice_fusion
  (28 shorter events, 1.1 us)
Async XLA Ops:
  7.4 93.9 %all-gather.9.cloned.1.call-start = ((), (), s32[]{:S(2)}) async-start(), calls=%async_computation.3 | async-start | bytes 10485760 | tf_op jit(solution)/shard_map/all_gather | solution.py:18
  101.3 323.7 %all-to-all-start = ((f32[512,4,1024]{0,2,1:T(8,128)}), f32[512,4,1024]{0,2,1:T(8,128)}, u32[]{:S(2)}, u32[]{:S(2)}) async-start(f32[512,4,1024]{0,2,1:T(8,128)} %bitcast.14), calls=%async_computation | async-start | bytes 16777216 | tf_op jit(solution)/shard_map/all_to_all | solution.py:19
  107.0 326.8 %all-gather.11.cloned.1.call-start = ((), (), s32[]{:S(2)}) async-start(), calls=%async_computation.4 | async-start | bytes 10485760 | tf_op jit(solution)/shard_map/all_gather | solution.py:23
  110.2 381.6 %all-reduce.4.cloned.1.call-start = ((), (), s32[]{:S(2)}) async-start(), calls=%async_computation.5 | async-start | bytes 8388608 | tf_op jit(solution)/shard_map/psum | solution.py:28
  465.4 3.2 copy-start
  465.5 3.2 copy-start.1
  465.5 116.9 %all-gather.7.cloned.1.call-start = ((), (), s32[]{:S(2)}) async-start(), calls=%async_computation.2 | async-start | bytes 10485760 | tf_op jit(solution)/shard_map/all_gather | solution.py:46
  468.6 264.8 %all-gather.13.cloned.1.call-start = ((), (), s32[]{:S(2)}) async-start(), calls=%async_computation.6 | async-start | bytes 10485760 | tf_op jit(solution)/shard_map/all_gather | solution.py:50
  495.2 296.5 %all-reduce.6.cloned.1.call-start = ((), (), s32[]{:S(2)}) async-start(), calls=%async_computation.7 | async-start | bytes 8388608 | tf_op jit(solution)/shard_map/psum | solution.py:54
  765.3 149.7 %all-gather.17.cloned.1.call-start = ((), (), s32[]{:S(2)}) async-start(), calls=%async_computation.9 | async-start | bytes 10485760 | tf_op jit(solution)/shard_map/all_gather | solution.py:56
  765.9 316.9 %all-gather.15.cloned.1.call-start = ((), (), s32[]{:S(2)}) async-start(), calls=%async_computation.8 | async-start | bytes 10485760 | tf_op jit(solution)/shard_map/all_gather | solution.py:60
  794.9 345.2 %all-reduce.8.cloned.1.call-start = ((), (), s32[]{:S(2)}) async-start(), calls=%async_computation.10 | async-start | bytes 8388608 | tf_op jit(solution)/shard_map/psum | solution.py:66
Sparse Core Ops, SparseCore 0:
  11.1 90.1 all-gather.8
  465.6 26.2 all-reduce.3
  493.7 88.6 all-gather.6
  583.8 149.5 all-gather.12
  765.4 26.2 all-reduce.5
  1114.8 25.3 all-reduce.7
Sparse Core Ops, SparseCore 1:
  110.3 293.4 all-gather.10
  767.4 147.6 all-gather.16
  916.8 165.9 all-gather.14
where the time goes:
time: 1150 us
  waiting for transfers between devices  838 us (73%)
  blocking collectives  159 us (14%)
  matrix products  95.3 us (8%)
  local copies, waits for them, and re-layouts  34.4 us (3%)
  between operations  15.2 us (1%)
    all_to_all x1, waiting for transfers between devices, on_device(): lax.all_to_all(row_strip, 'row', split_axis=1, concat_axis=0, tiled=True)  315 us
    all_to_all x1, blocking collectives, on_device(): lax.all_to_all(column_slab, 'col', split_axis=0, concat_axis=1, tiled=True)  159 us
    all_gather x1, waiting for transfers between devices, on_device(): lax.all_gather(scaled, 'row', axis=0, tiled=True)  151 us
    all_gather x1, waiting for transfers between devices, on_device(): column_slab = lax.all_gather(u_right, 'row', axis=0, tiled=True)  120 us
    all_gather x1, waiting for transfers between devices, on_device(): row_strip = lax.all_gather(u_top, 'col', axis=1, tiled=True)  90.4 us
    all_gather x1, waiting for transfers between devices, on_device(): u_strip = lax.all_gather(u_right, 'col', axis=1, tiled=True)  86.9 us
    dot_general x1, matrix products, on_device(): jnp.dot(section, lax.all_gather(scaled, 'row', axis=0, tiled=True), preci...  31.8 us
    dot_general x1, matrix products, on_device(): lax.dot_general(lax.all_gather(left_half, 'col', axis=1, tiled=True), sec...  31.8 us
  transfers between devices with their start and end apart: 10, of which 9 were waited for; matrix products, arithmetic and copies ran while one was open for 3% of the time, Pallas kernels for 0%

commit v1 on v0

--- a/solution.py
+++ b/solution.py
@@ -2,6 +2,19 @@
 import jax.numpy as jnp
 from jax import lax
 from jax.sharding import PartitionSpec as P
+from jax.lax import axis_index, axis_size, ppermute
+
+
+def wrap_spot(block_in, along_axis):
+    how_many = axis_size(along_axis)
+    z1 = sorted(((ix, (ix + 1) % how_many) for ix in range(how_many)))
+    value_now = block_in
+    sheets = [value_now]
+    for tick in range(1, how_many):
+        value_now = ppermute(value_now, along_axis, z1)
+        sheets.insert(0, value_now)
+    found_now = jnp.concatenate(sheets, axis=1)
+    return jnp.roll(found_now, (axis_index(along_axis) + 1) * block_in.shape[1], axis=1)
 
 
 def on_device(basis, basis_grad, value_grad, ranks, offsets):
@@ -43,7 +56,7 @@
         inner_half / jnp.where(on_diagonal, jnp.float32(1.0), spacing),
     )
     u_right = lax.dynamic_slice_in_dim(basis, layer_id * half_cols, half_cols, 1)
-    u_strip = lax.all_gather(u_right, "col", axis=1, tiled=True)
+    u_strip = wrap_spot(u_right, "col")
     section = u_strip
     left_prod = jnp.dot(
         section,

time: 1150 us -> 1080 us (0.939)
  waiting for transfers between devices: 838 us -> 746 us
  local copies, waits for them, and re-layouts: 34.4 us -> 53.6 us
    all_gather x1, waiting for transfers between devices: 151 us -> 0.01 us  [on_device(): lax.all_gather(scaled, 'row', axis=0, tiled=True)]
    ppermute x0 -> x3, waiting for transfers between devices: none -> 142 us  [wrap_spot(): value_now = ppermute(value_now, along_axis, z1)]
    all_gather x1 -> x0, waiting for transfers between devices: 86.9 us -> none  [on_device(): u_strip = lax.all_gather(u_right, 'col', axis=1, tiled=True)]
    unnamed x5 -> x20, local copies, waits for them, and re-layouts: 1.83 us -> 20.9 us
  transfers between devices with their start and end apart: 10 -> 12, of which waited for: 9 -> 10; matrix products, arithmetic and copies ran while one was open for 3% -> 4% of each run, Pallas kernels for 0% -> 0%
where the time goes in v1:
time: 1080 us
  waiting for transfers between devices  746 us (69%)
  blocking collectives  159 us (15%)
  matrix products  95.3 us (9%)
  local copies, waits for them, and re-layouts  53.6 us (5%)
  between operations  14.9 us (1%)
    all_to_all x1, waiting for transfers between devices, on_device(): lax.all_to_all(row_strip, 'row', split_axis=1, concat_axis=0, tiled=True)  315 us
    all_to_all x1, blocking collectives, on_device(): lax.all_to_all(column_slab, 'col', split_axis=0, concat_axis=1, tiled=True)  159 us
    ppermute x3, waiting for transfers between devices, wrap_spot(): value_now = ppermute(value_now, along_axis, z1)  142 us
    all_gather x1, waiting for transfers between devices, on_device(): column_slab = lax.all_gather(u_right, 'row', axis=0, tiled=True)  120 us
    all_gather x1, waiting for transfers between devices, on_device(): row_strip = lax.all_gather(u_top, 'col', axis=1, tiled=True)  90.4 us
    dot_general x1, matrix products, on_device(): jnp.dot(section, lax.all_gather(scaled, 'row', axis=0, tiled=True), preci...  31.9 us
    dot_general x1, matrix products, on_device(): lax.dot_general(lax.all_gather(left_half, 'col', axis=1, tiled=True), sec...  31.8 us
    dot_general x1, matrix products, on_device(): lax.dot_general(section, lax.all_gather(du_top, 'row', axis=0, tiled=True...  31.6 us
  transfers between devices with their start and end apart: 12, of which 10 were waited for; matrix products, arithmetic and copies ran while one was open for 4% of the time, Pallas kernels for 0%

profile of v1, /device:TPU:0, one launch (start us, length us, event | category | flops | bytes accessed | tf_op | source)
XLA Modules:
  0.0 1080.7 jit_solution(4285743129014713352)
XLA Ops:
  10.9 90.4 %all-gather.6.cloned.1.call-done = f32[512,4096]{0,1:T(8,128)} async-done(((f32[512,1024]{0,1:T(8,128)}), f32[512,4096]{0,1:T(8,128)}) %all-gather.6.cloned.1.call-update) | async-done | bytes 8388624 | tf_op jit(solution)/shard_map/all_gather | solution.py:31
  101.3 5.7 all-to-all-start
  107.1 3.2 constant_dynamic-slice_fusion.2
  110.3 314.7 %all-to-all-done = f32[512,4,1024]{0,2,1:T(8,128)} async-done(((f32[512,4,1024]{0,2,1:T(8,128)}), f32[512,4,1024]{0,2,1:T(8,128)}, u32[]{:S(2)}, u32[]{:S(2)}) %all-to-all-start) | async-done | bytes 8388640 | tf_op jit(solution)/shard_map/all_to_all | solution.py:32
  425.0 8.8 copy.7
  433.8 31.6 %fusion.4 = f32[1024,1024]{1,0:T(8,128)} fusion(f32[2048,1024]{1,0:T(8,128)} %bitcast.14, f32[2048,1024]{1,0:T(8,128)} %all-gather.8.cloned.1.call-done), kind=kOutput, calls=%fused_computation.22 | convolution fusion | flops 25769803776 | bytes 20971520 | tf_op jit(solution)/shard_map/dot_general | solution.py:34
  466.9 24.9 %all-reduce.4.cloned.1.call-done = f32[1024,1024]{1,0:T(8,128)} async-done(((f32[1024,1024]{1,0:T(8,128)}), f32[1024,1024]{1,0:T(8,128)}) %all-reduce.4.cloned.1.call-update) | async-done | bytes 4194320 | tf_op jit(solution)/shard_map/psum | solution.py:41
  491.8 3.4 compare_select_fusion
  498.9 47.0 %collective-permute-done = f32[1024,512]{1,0:T(8,128)S(1)} collective-permute-done((f32[1024,512]{1,0:T(8,128)S(1)}, f32[1024,512]{1,0:T(8,128)S(1)}, u32[]{:S(2)}, u32[]{:S(2)}) %collective-permute-start) | collective-permute-done | bytes 2097184 | tf_op jit(solution)/shard_map/ppermute | solution.py:14
  548.0 47.3 %collective-permute-done.1 = f32[1024,512]{1,0:T(8,128)} collective-permute-done((f32[1024,512]{1,0:T(8,128)S(1)}, f32[1024,512]{1,0:T(8,128)}, u32[]{:S(2)}, u32[]{:S(2)}) %collective-permute-start.1) | collective-permute-done | bytes 2097184 | tf_op jit(solution)/shard_map/ppermute | solution.py:14
  595.3 47.4 %collective-permute-done.2 = f32[1024,512]{1,0:T(8,128)} collective-permute-done((f32[1024,512]{1,0:T(8,128)}, f32[1024,512]{1,0:T(8,128)}, u32[]{:S(2)}, u32[]{:S(2)}) %collective-permute-start.2) | collective-permute-done | bytes 2097184 | tf_op jit(solution)/shard_map/ppermute | solution.py:14
  642.7 3.1 constant_dynamic-update-slice_fusion.7
  645.8 3.2 constant_dynamic-update-slice_fusion.6
  652.1 3.1 constant_dynamic-update-slice_fusion.3
  655.2 3.2 constant_dynamic-update-slice_fusion.2
  661.4 31.9 %fusion = f32[1024,1024]{1,0:T(8,128)} fusion(f32[2048,1024]{1,0:T(8,128)} %all-gather.10.cloned.1.call-done, f32[1024,4096]{1,0:T(8,128)} %constant_dynamic-update-slice_fusion, s32[]{:T(128)S(6)} %select_n.38), kind=kOutput, calls=%fused_computation | convolution fusion | flops 25769803776 | bytes 20971524 | tf_op jit(solution)/shard_map/dot_general | solution.py:61
  693.9 28.0 %all-reduce.6.cloned.1.call-done = f32[1024,1024]{1,0:T(8,128)} async-done(((f32[1024,1024]{1,0:T(8,128)}), f32[1024,1024]{1,0:T(8,128)}) %all-reduce.6.cloned.1.call-update) | async-done | bytes 4194320 | tf_op jit(solution)/shard_map/psum | solution.py:67
  721.9 3.1 constant_dynamic-slice_fusion.1
  725.1 120.0 %all-gather.14.cloned.1.call-done = f32[4096,512]{1,0:T(8,128)} async-done(((f32[1024,512]{1,0:T(8,128)}), f32[4096,512]{1,0:T(8,128)}) %all-gather.14.cloned.1.call-update) | async-done | bytes 8388624 | tf_op jit(solution)/shard_map/all_gather | solution.py:69
  845.1 158.6 %all_to_all.38 = f32[4,1024,512]{2,1,0:T(8,128)} all-to-all(f32[4,1024,512]{2,1,0:T(8,128)} %bitcast.12), channel_id=1, replica_groups=mesh['row'=4,'col'=4,'layer'=2] {'col'}, dimensions={0} | all-to-all | bytes 16777216 | tf_op jit(solution)/shard_map/all_to_all | solution.py:70
  1003.7 8.7 copy.8
  1012.8 31.8 %fusion.5 = f32[1024,1024]{1,0:T(8,128)} fusion(f32[1024,2048]{1,0:T(8,128)} %all-gather.12.cloned.1.call-done, f32[1024,2048]{0,1:T(8,128)} %bitcast.15), kind=kOutput, calls=%fused_computation.23 | convolution fusion | flops 25769803776 | bytes 20971520 | tf_op jit(solution)/shard_map/dot_general | solution.py:72
  1044.7 25.5 %all-reduce.8.cloned.1.call-done = f32[1024,1024]{1,0:T(8,128)} async-done(((f32[1024,1024]{1,0:T(8,128)}), f32[1024,1024]{1,0:T(8,128)}) %all-reduce.8.cloned.1.call-update) | async-done | bytes 4194320 | tf_op jit(solution)/shard_map/psum | solution.py:79
  1070.2 3.2 constant_dynamic-slice_fusion
  (47 shorter events, 18.2 us)
Async XLA Ops:
  7.4 93.9 %all-gather.6.cloned.1.call-start = ((), (), s32[]{:S(2)}) async-start(), calls=%async_computation.2 | async-start | bytes 10485760 | tf_op jit(solution)/shard_map/all_gather | solution.py:31
  101.3 323.7 %all-to-all-start = ((f32[512,4,1024]{0,2,1:T(8,128)}), f32[512,4,1024]{0,2,1:T(8,128)}, u32[]{:S(2)}, u32[]{:S(2)}) async-start(f32[512,4,1024]{0,2,1:T(8,128)} %bitcast.13), calls=%async_computation | async-start | bytes 16777216 | tf_op jit(solution)/shard_map/all_to_all | solution.py:32
  107.0 326.8 %all-gather.8.cloned.1.call-start = ((), (), s32[]{:S(2)}) async-start(), calls=%async_computation.3 | async-start | bytes 10485760 | tf_op jit(solution)/shard_map/all_gather | solution.py:36
  110.3 381.6 %all-reduce.4.cloned.1.call-start = ((), (), s32[]{:S(2)}) async-start(), calls=%async_computation.4 | async-start | bytes 8388608 | tf_op jit(solution)/shard_map/psum | solution.py:41
  465.4 0.7 copy-start.4
  465.4 0.7 copy-start.5
  465.4 195.9 %all-gather.10.cloned.1.call-start = ((), (), s32[]{:S(2)}) async-start(), calls=%async_computation.5 | async-start | bytes 10485760 | tf_op jit(solution)/shard_map/all_gather | solution.py:63
  495.3 226.7 %all-reduce.6.cloned.1.call-start = ((), (), s32[]{:S(2)}) async-start(), calls=%async_computation.6 | async-start | bytes 8388608 | tf_op jit(solution)/shard_map/psum | solution.py:67
  497.1 152.0 %copy-start.1 = (f32[1024,512]{1,0:T(8,128)}, f32[1024,512]{1,0:T(8,128)S(1)}, u32[]{:S(2)}) copy-start(f32[1024,512]{1,0:T(8,128)S(1)} %constant_dynamic-slice_fusion.4) | copy-start | bytes 6291460
  497.1 48.8 %collective-permute-start = (f32[1024,512]{1,0:T(8,128)S(1)}, f32[1024,512]{1,0:T(8,128)S(1)}, u32[]{:S(2)}, u32[]{:S(2)}) collective-permute-start(f32[1024,512]{1,0:T(8,128)S(1)} %constant_dynamic-slice_fusion.4), channel_id=1, source_target_pairs={{0,2},{2,4},{4,6},{6,0},{1,3},{3,5},{5,7},{7,1},{8,10},{10,12},{12... | collective-permute-start | bytes 6291464 | tf_op jit(solution)/shard_map/ppermute | solution.py:14
  545.9 1.3 copy-start.2
  547.2 48.1 %collective-permute-start.1 = (f32[1024,512]{1,0:T(8,128)S(1)}, f32[1024,512]{1,0:T(8,128)}, u32[]{:S(2)}, u32[]{:S(2)}) collective-permute-start(f32[1024,512]{1,0:T(8,128)S(1)} %collective-permute-done), channel_id=1, source_target_pairs={{0,2},{2,4},{4,6},{6,0},{1,3},{3,5},{5,7},{7,1},{8,10},{10,12},{12... | collective-permute-start | bytes 6291464 | tf_op jit(solution)/shard_map/ppermute | solution.py:14
  595.3 47.4 %collective-permute-start.2 = (f32[1024,512]{1,0:T(8,128)}, f32[1024,512]{1,0:T(8,128)}, u32[]{:S(2)}, u32[]{:S(2)}) collective-permute-start(f32[1024,512]{1,0:T(8,128)} %collective-permute-done.1), channel_id=1, source_target_pairs={{0,2},{2,4},{4,6},{6,0},{1,3},{3,5},{5,7},{7,1},{8,10},{10,12},{12... | collective-permute-start | bytes 6291464 | tf_op jit(solution)/shard_map/ppermute | solution.py:14
  595.3 53.7 %copy-start.3 = (f32[1024,512]{1,0:T(8,128)S(1)}, f32[1024,512]{1,0:T(8,128)}, u32[]{:S(2)}) copy-start(f32[1024,512]{1,0:T(8,128)} %copy-done.2) | copy-start | bytes 6291460
  645.8 4.7 copy-start
  693.3 151.8 %all-gather.14.cloned.1.call-start = ((), (), s32[]{:S(2)}) async-start(), calls=%async_computation.8 | async-start | bytes 10485760 | tf_op jit(solution)/shard_map/all_gather | solution.py:69
  693.9 318.9 %all-gather.12.cloned.1.call-start = ((), (), s32[]{:S(2)}) async-start(), calls=%async_computation.7 | async-start | bytes 10485760 | tf_op jit(solution)/shard_map/all_gather | solution.py:73
  725.1 345.1 %all-reduce.8.cloned.1.call-start = ((), (), s32[]{:S(2)}) async-start(), calls=%async_computation.9 | async-start | bytes 8388608 | tf_op jit(solution)/shard_map/psum | solution.py:79
Sparse Core Ops, SparseCore 0:
  11.1 90.1 all-gather.5
  465.6 26.2 all-reduce.3
  693.4 28.4 all-reduce.5
  1044.8 25.3 all-reduce.7
Sparse Core Ops, SparseCore 1:
  110.3 293.4 all-gather.7
  495.3 150.6 all-gather.9
  695.3 149.7 all-gather.13
  847.0 165.8 all-gather.11
